TPU v7x, 256 devices: a 4x2x16 block of a 4x16x16 slice. The times are simulated.
256 devices in a mesh: groups: 2 (over y), fsdp: 32 (over z, core), expert: 4 (over x).
Axes of the slice: x: 4, y: 2, z: 16, core: 2. Of those that a mesh axis runs over, the one named last changes fastest.
The devices are a block of a 4x16x16 slice.
Arguments:
- queries: bfloat16 [4096, 2048], P(('groups', 'fsdp'), 'expert'), parts along dimension 0, may hold values from -14 to 14
- keys: bfloat16 [64, 2048, 512], P(('groups', 'fsdp'), None, 'expert'), parts along dimension 0, may hold values from -14 to 14
- values: bfloat16 [64, 2048, 512], P(('groups', 'fsdp'), None, 'expert'), parts along dimension 0, may hold values from -4 to 4
- out_weight: bfloat16 [2048, 4096], P('expert', 'fsdp'), may hold values from -0.5 to 0.5
- residual: bfloat16 [4096, 4096], P(('groups', 'fsdp')), parts along dimension 0, may hold values from -3 to 3
- norm_gain: float32 [4096], replicated, may hold values from 0.5 to 1.5
- route_ids: int32 [4096, 2], P(('groups', 'fsdp')), parts along dimension 0, may hold values from 0 to 7, as said below
- route_slots: int32 [4096, 2], P(('groups', 'fsdp')), parts along dimension 0, may hold values from 0 to 23, as said below
- route_weights: int32 [4096, 2], P(('groups', 'fsdp')), parts along dimension 0, may hold values from 1 to 65535, as said below
- w_gate: bfloat16 [8, 4096, 7168], P('expert', None, 'fsdp'), may hold values from -0.09375 to 0.09375
- w_up: bfloat16 [8, 4096, 7168], P('expert', None, 'fsdp'), may hold values from -0.09375 to 0.09375
- w_down: bfloat16 [8, 7168, 4096], P('expert', 'fsdp'), may hold values from -0.0625 to 0.0625
Outputs:
- layer_out: bfloat16 [4096, 4096], P(('groups', 'fsdp'), 'expert'), parts along dimension 0
There are 2 independent parts, one for each index of `groups`. A program takes and returns all parts, laid end to end along the dimension named above; an argument that names none is the same for every part. Nothing has to cross between parts.
Inputs may be any that keep to these rules, and one draw needn't show every extreme that they name: `route_ids`: each row names two different experts. Among the rows of one block, no expert is named more than 24 times and no group of experts 2 g and 2 g + 1 more than 36 times; one expert, the same for all blocks, is named exactly 24 times in every block and its group exactly 36 times; every expert is named in every block. `route_slots`: within one block, the routes to one expert hold the slots 0 to their count - 1, each once. `route_weights`: the two entries of a row sum to 65536.
All inputs are finite; a program needn't handle non-finite values.
Results may differ from a plain program's by a relative error of at most 0.02.
Values may be sent and summed in bfloat16 or wider, within the bound.
A program may use at most 128 MiB of HBM per device.

v0:
```python
import jax
import jax.numpy as jnp
from jax import lax
from jax.sharding import PartitionSpec as P

HEAD_DIM = 128
GCAP = 36
eps = 1e-05


def copy_for_each(shard, axis):
    copies = jnp.broadcast_to(shard, (lax.axis_size(axis), *shard.shape))
    return lax.all_to_all(copies, axis, split_axis=0, concat_axis=0, tiled=True)


def taken_together(shard, axis):
    everything = copy_for_each(shard, axis)
    return jnp.sum(everything.astype(jnp.float32), axis=0)


def sent_together(arrays, axis, dim, along):
    columns = [a.reshape(*a.shape[:along], -1) for a in arrays]
    both = jnp.concatenate(columns, axis=along)
    result, at, outs = (lax.all_gather(both, axis, axis=dim, tiled=True), 0, [])
    for a, column in zip(arrays, columns):
        slab = result[..., at : at + column.shape[along]]
        outs.append(slab.reshape(*slab.shape[:along], *a.shape[along:]))
        at += column.shape[along]
    return tuple(outs)


def in_blocks(shard, dim, peers):
    before, after = (shard.shape[:dim], shard.shape[dim + 1 :])
    return jnp.moveaxis(shard.reshape(*before, peers, -1, *after), dim, 0)


def summed_on_arrival(shard, axis, dim):
    peers = lax.axis_size(axis)
    pieces = lax.all_to_all(in_blocks(shard, dim, peers), axis, 0, 0, tiled=True)
    return jnp.sum(pieces.astype(jnp.float32), axis=0)


def attend(queries, keys, values):
    block = queries.shape[0]
    context = keys.shape[1]
    kv_dev = keys.shape[2] // HEAD_DIM
    heads_dev = queries.shape[1] // HEAD_DIM
    group = heads_dev // kv_dev
    query_heads = queries.reshape(block, kv_dev, group, HEAD_DIM)
    key_heads = keys[0].reshape(context, kv_dev, HEAD_DIM)
    value_heads = values[0].reshape(context, kv_dev, HEAD_DIM)
    scores = jnp.einsum(
        "qcgd,kcd->cgqk", query_heads, key_heads, preferred_element_type=jnp.float32
    ) * HEAD_DIM ** (-0.5)
    key_pos = jnp.arange(context)
    query_pos = context - block + jnp.arange(block)
    allowed = key_pos[None, :] <= query_pos[:, None]
    masked = jnp.where(allowed, scores, -1e30)
    highest = jnp.max(masked, axis=-1, keepdims=True)
    weights = jnp.where(allowed, jnp.exp(masked - highest), 0.0)
    probs = (weights / jnp.sum(weights, axis=-1, keepdims=True)).astype(jnp.bfloat16)
    heads_out = jnp.einsum("cgqk,kcd->qcgd", probs, value_heads, preferred_element_type=jnp.float32)
    return heads_out.astype(jnp.bfloat16).reshape(block, heads_dev * HEAD_DIM)


def per_device(
    queries,
    keys,
    values,
    out_weight,
    residual,
    norm_gain,
    route_ids,
    route_slots,
    route_weights,
    w_gate,
    w_up,
    w_down,
):
    heads_out = attend(queries, keys, values)
    partial_attn = jnp.dot(
        heads_out,
        lax.all_gather(out_weight, "fsdp", axis=1, tiled=True),
        preferred_element_type=jnp.float32,
    )
    attn = taken_together(partial_attn.astype(jnp.bfloat16), "expert").astype(jnp.float32)
    hstate = (residual.astype(jnp.float32) + attn).astype(jnp.bfloat16)
    state = hstate.astype(jnp.float32)
    scale = lax.rsqrt(jnp.mean(state * state, axis=-1, keepdims=True) + eps)
    normed = (state * scale * norm_gain).astype(jnp.bfloat16)
    group_index = lax.axis_index("expert")
    first_expert = 2 * group_index
    within = route_ids - first_expert
    in_group = (within >= 0) & (within < 2)
    lead_count = jnp.sum((route_ids == first_expert).astype(jnp.int32))
    target = jnp.where(in_group, route_slots + within * lead_count, -1)
    row_ids = jnp.arange(GCAP)
    one_hot = (
        (target[None, :, 0] == row_ids[:, None]) | (target[None, :, 1] == row_ids[:, None])
    ).astype(jnp.bfloat16)
    dispatch = jnp.dot(one_hot, normed, preferred_element_type=jnp.float32).astype(jnp.bfloat16)
    second = (row_ids >= lead_count).astype(jnp.bfloat16)
    rows, labels = sent_together((dispatch, second), "fsdp", 0, 1)
    gate = jnp.einsum("nd,edf->enf", rows, w_gate, preferred_element_type=jnp.float32)
    upper = jnp.einsum("nd,edf->enf", rows, w_up, preferred_element_type=jnp.float32)
    labels_f = labels.astype(jnp.float32)
    keep = jnp.stack([1.0 - labels_f, labels_f], axis=0)[:, :, None]
    values_new = (jax.nn.silu(gate) * upper * keep).astype(jnp.bfloat16)
    flat_out = lax.psum_scatter(
        jnp.einsum("enf,efd->nd", values_new, w_down, preferred_element_type=jnp.float32).astype(
            jnp.bfloat16
        ),
        "fsdp",
        scatter_dimension=0,
        tiled=True,
    ).astype(jnp.float32)
    row_index = route_slots + within * lead_count
    safe_index = jnp.where(in_group, row_index, 0)
    shares = jnp.where(in_group, route_weights.astype(jnp.float32) / 65536.0, 0.0)
    picked = jnp.take(flat_out, safe_index, axis=0)
    contrib = jnp.sum(shares[:, :, None] * picked, axis=1)
    moe = summed_on_arrival(contrib.astype(jnp.bfloat16), "expert", 1)
    width = moe.shape[1]
    own_state = lax.dynamic_slice_in_dim(hstate, group_index * width, width, 1)
    return (own_state.astype(jnp.float32) + moe).astype(jnp.bfloat16)


def solution(mesh):
    in_specs = (
        P(("groups", "fsdp"), "expert"),
        P(("groups", "fsdp"), None, "expert"),
        P(("groups", "fsdp"), None, "expert"),
        P("expert", "fsdp"),
        P(("groups", "fsdp"), None),
        P(),
        P(("groups", "fsdp"), None),
        P(("groups", "fsdp"), None),
        P(("groups", "fsdp"), None),
        P("expert", None, "fsdp"),
        P("expert", None, "fsdp"),
        P("expert", "fsdp", None),
    )
    out_specs = P(("groups", "fsdp"), "expert")
    return jax.shard_map(
        per_device, mesh=mesh, in_specs=in_specs, out_specs=out_specs, check_vma=False
    )
```

profile of v0, /device:TPU:417, one launch (start us, length us, event | category | flops | bytes accessed | tf_op | source)
XLA Modules:
  0.0 382.8 jit_solution(10625348687652536732)
XLA Ops:
  7.6 1.5 fusion.33
  10.4 86.3 %all-gather.4.cloned.1.call-done = bf16[512,4096]{1,0:T(8,128)(2,1)} async-done(((bf16[512,128]{1,0:T(8,128)(2,1)}), bf16[512,4096]{1,0:T(8,128)(2,1)}) %all-gather.4.cloned.1.call-update) | async-done | bytes 4194320 | tf_op jit(solution)/shard_map/all_gather | solution.py:83
  96.8 3.0 convolution_convert_fusion
  99.8 1.6 broadcast_in_dim.51
  101.4 4.1 %all-to-all-start = ((bf16[4,64,4096]{2,1,0:T(8,128)(2,1)}), bf16[4,64,4096]{2,1,0:T(8,128)(2,1)S(1)}, u32[]{:S(2)}, u32[]{:S(2)}) async-start(bf16[4,64,4096]{2,1,0:T(8,128)(2,1)} %broadcast_in_dim.51), calls=%async_computation | async-start | bytes 4194304 | tf_op jit(solution)/shard_map/all_to_all | solution.py:13
  107.6 23.8 %all-to-all-done = bf16[4,64,4096]{2,1,0:T(8,128)(2,1)S(1)} async-done(((bf16[4,64,4096]{2,1,0:T(8,128)(2,1)}), bf16[4,64,4096]{2,1,0:T(8,128)(2,1)S(1)}, u32[]{:S(2)}, u32[]{:S(2)}) %all-to-all-start) | async-done | bytes 2097184 | tf_op jit(solution)/shard_map/all_to_all | solution.py:13
  133.2 76.2 %all-gather.6.cloned.1.call-done = bf16[32,36,4097]{2,1,0:T(8,128)(2,1)} async-done(((bf16[1,36,4097]{2,1,0:T(8,128)(2,1)}), bf16[32,36,4097]{2,1,0:T(8,128)(2,1)}) %all-gather.6.cloned.1.call-update) | async-done | bytes 9439504 | tf_op jit(solution)/shard_map/all_gather | solution.py:24
  209.4 14.2 %reshape.107 = bf16[1152,4097]{1,0:T(8,128)(2,1)} reshape(bf16[32,36,4097]{2,1,0:T(8,128)(2,1)} %all-gather.6.cloned.1.call-done) | data formatting | bytes 18878976
  224.8 9.8 %fusion.3 = f32[1152,448]{0,1:S(1)} fusion(bf16[4096,448]{0,1:T(8,128)(2,1)} %bitcast.70, bf16[1152,4097]{1,0:T(8,128)(2,1)} %reshape.107), kind=kOutput, calls=%fused_computation.4 | convolution fusion | flops 4227858432 | bytes 15171584
  234.6 4.9 %fusion.1 = f32[1152,448]{0,1:S(1)} fusion(bf16[4096,448]{0,1:T(8,128)(2,1)S(1)} %bitcast.71, bf16[1152,4097]{1,0:T(8,128)(2,1)S(1)} %copy-done.2), kind=kOutput, calls=%fused_computation.2 | convolution fusion | flops 4227858432 | bytes 15171584
  239.6 7.6 %bitcast_convert_fusion = bf16[1152,4096]{1,0:T(8,128)(2,1)} fusion(bf16[2,224,4096]{2,1,0:T(8,128)(2,1)S(1)} %copy-done.10, f32[2,1152,224]{1,2,0:T(8,128)S(1)} %bitcast.73, f32[2,1152,224]{1,2,0:T(8,128)S(1)} %bitcast.72, f32[2,1152]{1,0:T(2,128)S(1)} %pad_maximum_fusion), kind=kOutput, calls=%fused_computation.1 | convolution fusion | flops 4236189696 | bytes 17245184 | tf_op jit(solution)/shard_map/enf,efd->nd/dot_general | solution.py:110
  247.2 72.3 %fusion = bf16[40,4096]{1,0:T(8,128)(2,1)S(1)} fusion(bf16[1152,4096]{1,0:T(8,128)(2,1)} %bitcast_convert_fusion), kind=kCustom, calls=%all-reduce-scatter | all-reduce-scatter fusion | flops 5242881 | bytes 9765888
  319.6 5.8 %collective-permute-start = (bf16[40,4096]{1,0:T(8,128)(2,1)S(1)}, bf16[40,4096]{1,0:T(8,128)(2,1)S(1)}, u32[]{:S(2)}, u32[]{:S(2)}) collective-permute-start(bf16[40,4096]{1,0:T(8,128)(2,1)S(1)} %fusion), channel_id=1, source_target_pairs={{0,4},{4,8},{8,12},{12,16},{16,20},{20,24},{24,28},{28,32},{32,36}... | collective-permute-start | bytes 983048
  325.4 2.0 collective-permute-start.1
  327.4 2.0 collective-permute-start.2
  330.3 5.3 %collective-permute-start.3 = (bf16[4,4096]{1,0:T(4,128)(2,1)S(1)}, bf16[4,4096]{1,0:T(4,128)(2,1)S(1)}, u32[]{:S(2)}, u32[]{:S(2)}) collective-permute-start(bf16[4,4096]{1,0:T(4,128)(2,1)S(1)} %slice.20), channel_id=1, source_target_pairs={{0,16},{4,20},{8,24},{12,28},{16,32},{20,36},{24,40},{28,44},{32,4... | collective-permute-start | bytes 98312
  337.0 11.4 %collective-permute-done.3 = bf16[4,4096]{1,0:T(4,128)(2,1)S(1)} collective-permute-done((bf16[4,4096]{1,0:T(4,128)(2,1)S(1)}, bf16[4,4096]{1,0:T(4,128)(2,1)S(1)}, u32[]{:S(2)}, u32[]{:S(2)}) %collective-permute-start.3) | collective-permute-done | bytes 32800
  348.4 1.7 concatenate.4
  350.1 1.3 gather_fusion
  351.5 2.3 reshape.97
  353.8 5.3 %multiply_reduce_fusion = bf16[64,4096]{1,0:T(8,128)(2,1)S(1)} fusion(f32[64,2,4096]{2,1,0:T(2,128)} %reshape.97, pred[64,2]{1,0:T(8,128)(4,1)S(1)} %copy.36, f32[64,2]{1,0:T(8,128)S(1)} %copy.35), kind=kLoop, calls=%fused_computation.12 | loop fusion | flops 1310720 | bytes 2622080 | tf_op jit(solution)/shard_map/reduce_sum | solution.py:121
  360.4 4.0 %all-to-all-start.1 = ((bf16[4,64,1024]{2,1,0:T(8,128)(2,1)}), bf16[4,64,1024]{2,1,0:T(8,128)(2,1)S(1)}, u32[]{:S(2)}, u32[]{:S(2)}) async-start(bf16[4,64,1024]{2,1,0:T(8,128)(2,1)} %copy.38), calls=%async_computation.1 | async-start | bytes 1048576 | tf_op jit(solution)/shard_map/all_to_all | solution.py:39
  364.3 9.9 %all-to-all-done.1 = bf16[4,64,1024]{2,1,0:T(8,128)(2,1)S(1)} async-done(((bf16[4,64,1024]{2,1,0:T(8,128)(2,1)}), bf16[4,64,1024]{2,1,0:T(8,128)(2,1)S(1)}, u32[]{:S(2)}, u32[]{:S(2)}) %all-to-all-start.1) | async-done | bytes 524320 | tf_op jit(solution)/shard_map/all_to_all | solution.py:39
  374.3 1.6 add_convert_fusion.1
  (64 shorter events, 10.5 us)
Async XLA Ops:
  6.5 1.0 copy-start
  6.6 90.2 %all-gather.4.cloned.1.call-start = ((), (), s32[]{:S(2)}) async-start(), calls=%async_computation.2 | async-start | bytes 4325376 | tf_op jit(solution)/shard_map/all_gather | solution.py:83
  7.6 2.0 copy-start.11
  101.4 4.2 %copy-start.5 = (s32[64,2]{0,1:T(2,128)S(1)}, s32[64,2]{0,1:T(2,128)}, u32[]{:S(2)}) copy-start(s32[64,2]{0,1:T(2,128)} %param.18) | copy-start | bytes 1540
  101.4 5.5 %copy-start.7 = (s32[64,2]{0,1:T(2,128)S(1)}, s32[64,2]{0,1:T(2,128)}, u32[]{:S(2)}) copy-start(s32[64,2]{0,1:T(2,128)} %param.20) | copy-start | bytes 1540
  101.4 5.5 %copy-start.6 = (s32[64,2]{0,1:T(2,128)S(1)}, s32[64,2]{0,1:T(2,128)}, u32[]{:S(2)}) copy-start(s32[64,2]{0,1:T(2,128)} %param.19) | copy-start | bytes 1540
  101.4 30.0 %all-to-all-start = ((bf16[4,64,4096]{2,1,0:T(8,128)(2,1)}), bf16[4,64,4096]{2,1,0:T(8,128)(2,1)S(1)}, u32[]{:S(2)}, u32[]{:S(2)}) async-start(bf16[4,64,4096]{2,1,0:T(8,128)(2,1)} %broadcast_in_dim.51), calls=%async_computation | async-start | bytes 4194304 | tf_op jit(solution)/shard_map/all_to_all | solution.py:13
  105.5 26.2 %copy-start.4 = (bf16[64,4096]{1,0:T(8,128)(2,1)S(1)}, bf16[64,4096]{1,0:T(8,128)(2,1)}, u32[]{:S(2)}) copy-start(bf16[64,4096]{1,0:T(8,128)(2,1)} %param.16) | copy-start | bytes 1572868
  105.5 103.8 %all-gather.6.cloned.1.call-start = ((), (), s32[]{:S(2)}) async-start(), calls=%async_computation.3 | async-start | bytes 11151360 | tf_op jit(solution)/shard_map/all_gather | solution.py:24
  107.6 24.5 %copy-start.12 = (f32[4096]{0:T(1024)S(1)}, f32[4096]{0:T(1024)}, u32[]{:S(2)}) copy-start(f32[4096]{0:T(1024)} %param.17) | copy-start | bytes 49156
  132.0 91.6 %copy-start.3 = (bf16[64,4096]{1,0:T(8,128)(2,1)}, bf16[64,4096]{1,0:T(8,128)(2,1)S(1)}, u32[]{:S(2)}) copy-start(bf16[64,4096]{1,0:T(8,128)(2,1)S(1)} %get-tuple-element.10) | copy-start | bytes 1572868
  224.7 9.8 %copy-start.2 = (bf16[1152,4097]{1,0:T(8,128)(2,1)S(1)}, bf16[1152,4097]{1,0:T(8,128)(2,1)}, u32[]{:S(2)}) copy-start(bf16[1152,4097]{1,0:T(8,128)(2,1)} %reshape.107) | copy-start | bytes 28318468
  224.8 9.8 %copy-start.9 = (bf16[2,4096,224]{1,2,0:T(8,128)(2,1)S(1)}, bf16[2,4096,224]{1,2,0:T(8,128)(2,1)}, u32[]{:S(2)}) copy-start(bf16[2,4096,224]{1,2,0:T(8,128)(2,1)} %param.22) | copy-start | bytes 11010052
  234.6 5.0 %copy-start.10 = (bf16[2,224,4096]{2,1,0:T(8,128)(2,1)S(1)}, bf16[2,224,4096]{2,1,0:T(8,128)(2,1)}, u32[]{:S(2)}) copy-start(bf16[2,224,4096]{2,1,0:T(8,128)(2,1)} %param.23) | copy-start | bytes 11010052
  247.2 88.6 %copy-start.8 = (u32[256]{0:T(256)S(1)}, u32[256]{0:T(256)}, u32[]{:S(2)}) copy-start(u32[256]{0:T(256)} %constant.60) | copy-start | bytes 3076
  319.6 28.8 %collective-permute-start = (bf16[40,4096]{1,0:T(8,128)(2,1)S(1)}, bf16[40,4096]{1,0:T(8,128)(2,1)S(1)}, u32[]{:S(2)}, u32[]{:S(2)}) collective-permute-start(bf16[40,4096]{1,0:T(8,128)(2,1)S(1)} %fusion), channel_id=1, source_target_pairs={{0,4},{4,8},{8,12},{12,16},{16,20},{20,24},{24,28},{28,32},{32,36}... | collective-permute-start | bytes 983048
  325.4 23.0 %collective-permute-start.1 = (bf16[40,4096]{1,0:T(8,128)(2,1)S(1)}, bf16[40,4096]{1,0:T(8,128)(2,1)S(1)}, u32[]{:S(2)}, u32[]{:S(2)}) collective-permute-start(bf16[40,4096]{1,0:T(8,128)(2,1)S(1)} %fusion), channel_id=1, source_target_pairs={{0,8},{4,12},{8,16},{12,20},{16,24},{20,28},{24,32},{28,36},{32,40... | collective-permute-start | bytes 983048
  327.4 21.0 %collective-permute-start.2 = (bf16[40,4096]{1,0:T(8,128)(2,1)S(1)}, bf16[40,4096]{1,0:T(8,128)(2,1)S(1)}, u32[]{:S(2)}, u32[]{:S(2)}) collective-permute-start(bf16[40,4096]{1,0:T(8,128)(2,1)S(1)} %fusion), channel_id=1, source_target_pairs={{0,12},{4,16},{8,20},{12,24},{16,28},{20,32},{24,36},{28,40},{32,4... | collective-permute-start | bytes 983048
  330.3 18.1 %collective-permute-start.3 = (bf16[4,4096]{1,0:T(4,128)(2,1)S(1)}, bf16[4,4096]{1,0:T(4,128)(2,1)S(1)}, u32[]{:S(2)}, u32[]{:S(2)}) collective-permute-start(bf16[4,4096]{1,0:T(4,128)(2,1)S(1)} %slice.20), channel_id=1, source_target_pairs={{0,16},{4,20},{8,24},{12,28},{16,32},{20,36},{24,40},{28,44},{32,4... | collective-permute-start | bytes 98312
  353.8 22.1 %copy-start.1 = (bf16[1,2048,128]{2,1,0:T(8,128)(2,1)S(1)}, bf16[1,2048,128]{2,1,0:T(8,128)(2,1)}, u32[]{:S(2)}) copy-start(bf16[1,2048,128]{2,1,0:T(8,128)(2,1)} %param.13) | copy-start | bytes 1572868
  360.4 13.9 %all-to-all-start.1 = ((bf16[4,64,1024]{2,1,0:T(8,128)(2,1)}), bf16[4,64,1024]{2,1,0:T(8,128)(2,1)S(1)}, u32[]{:S(2)}, u32[]{:S(2)}) async-start(bf16[4,64,1024]{2,1,0:T(8,128)(2,1)} %copy.38), calls=%async_computation.1 | async-start | bytes 1048576 | tf_op jit(solution)/shard_map/all_to_all | solution.py:39
Sparse Core Ops, SparseCore 0:
  9.1 87.5 all-gather.3
  133.3 76.0 all-gather.5
where the time goes:
time: 384 us; the launch traced here: 383 us
  waiting for transfers between devices  208 us (54%)
  blocking collectives  72.3 us (19%)
  matrix products  27.9 us (7%)
  local copies, waits for them, and re-layouts  23.7 us (6%)
  starting transfers between devices  23.1 us (6%)
  between operations  14.4 us (4%)
  other arithmetic  12.8 us (3%)
    all_gather x1, waiting for transfers between devices, per_device(): lax.all_gather(out_weight, 'fsdp', axis=1, tiled=True)  86.3 us
    all_gather x1, waiting for transfers between devices, sent_together(): result, at, outs = (lax.all_gather(both, axis, axis=dim, tiled=True), 0, [])  76.2 us
    unnamed x1, blocking collectives  72.3 us
    all_to_all x1, waiting for transfers between devices, copy_for_each(): return lax.all_to_all(copies, axis, split_axis=0, concat_axis=0, tiled=True)  23.8 us
    unnamed x30, local copies, waits for them, and re-layouts  16.7 us
    unnamed x4, starting transfers between devices  15 us
    unnamed x2, matrix products  14.7 us
    unnamed x6, waiting for transfers between devices  12.2 us
  transfers between devices with their start and end apart: 8, of which 5 were waited for; matrix products, arithmetic and copies ran while one was open for 2% of the time, Pallas kernels for 0%

commit v1 on v0

--- a/solution.py
+++ b/solution.py
@@ -1,11 +1,23 @@
+import functools
 import jax
 import jax.numpy as jnp
 from jax import lax
 from jax.sharding import PartitionSpec as P
+from jax.lax import all_to_all, axis_size
 
 HEAD_DIM = 128
 GCAP = 36
 eps = 1e-05
+
+
+def pass_the_row(x_part, k_dim):
+    parts_n = axis_size("fsdp")
+    in_order = [parts_n if kk == k_dim else 1 for kk in range(x_part.ndim)]
+    y = jnp.tile(x_part, in_order)
+    return all_to_all(y, "fsdp", tiled=True, concat_axis=k_dim, split_axis=k_dim)
+
+
+_connect_floor = functools.partial(pass_the_row, k_dim=1)
 
 
 def copy_for_each(shard, axis):
@@ -79,9 +91,7 @@
 ):
     heads_out = attend(queries, keys, values)
     partial_attn = jnp.dot(
-        heads_out,
-        lax.all_gather(out_weight, "fsdp", axis=1, tiled=True),
-        preferred_element_type=jnp.float32,
+        heads_out, _connect_floor(out_weight), preferred_element_type=jnp.float32
     )
     attn = taken_together(partial_attn.astype(jnp.bfloat16), "expert").astype(jnp.float32)
     hstate = (residual.astype(jnp.float32) + attn).astype(jnp.bfloat16)

time: 384 us -> 511 us (1.33)
  waiting for transfers between devices: 208 us -> 304 us
  starting transfers between devices: 23.1 us -> 44.5 us
  local copies, waits for them, and re-layouts: 23.7 us -> 34 us
    all_to_all x0 -> x1, waiting for transfers between devices: none -> 182 us  [pass_the_row(): all_to_all(y, 'fsdp', tiled=True, concat_axis=k_dim, split_axis=k_dim)]
    all_gather x1 -> x0, waiting for transfers between devices: 86.3 us -> none  [per_device(): lax.all_gather(out_weight, 'fsdp', axis=1, tiled=True)]
    all_to_all x0 -> x1, starting transfers between devices: none -> 21 us  [pass_the_row(): all_to_all(y, 'fsdp', tiled=True, concat_axis=k_dim, split_axis=k_dim)]
    all_to_all x0 -> x1, local copies, waits for them, and re-layouts: none -> 6.51 us  [pass_the_row(): all_to_all(y, 'fsdp', tiled=True, concat_axis=k_dim, split_axis=k_dim)]
    unnamed x6 -> x5, waiting for transfers between devices: 12.2 us -> 11.4 us
    unnamed x30 -> x32, local copies, waits for them, and re-layouts: 16.7 us -> 16.5 us
  transfers between devices with their start and end apart: 8 -> 8, of which waited for: 5 -> 5; matrix products, arithmetic and copies ran while one was open for 2% -> 1% of each run, Pallas kernels for 0% -> 0%
where the time goes in v1:
time: 511 us; the launch traced here: 510 us
  waiting for transfers between devices  304 us (59%)
  blocking collectives  72.3 us (14%)
  starting transfers between devices  44.5 us (9%)
  local copies, waits for them, and re-layouts  34 us (7%)
  matrix products  27.6 us (5%)
  between operations  14.4 us (3%)
  other arithmetic  12.8 us (3%)
    all_to_all x1, waiting for transfers between devices, pass_the_row(): all_to_all(y, 'fsdp', tiled=True, concat_axis=k_dim, split_axis=k_dim)  182 us
    all_gather x1, waiting for transfers between devices, sent_together(): result, at, outs = (lax.all_gather(both, axis, axis=dim, tiled=True), 0, [])  78.2 us
    unnamed x1, blocking collectives  72.3 us
    all_to_all x1, waiting for transfers between devices, copy_for_each(): return lax.all_to_all(copies, axis, split_axis=0, concat_axis=0, tiled=True)  22.7 us
    all_to_all x1, starting transfers between devices, pass_the_row(): all_to_all(y, 'fsdp', tiled=True, concat_axis=k_dim, split_axis=k_dim)  21 us
    unnamed x32, local copies, waits for them, and re-layouts  16.5 us
    unnamed x4, starting transfers between devices  15 us
    unnamed x2, matrix products  14.7 us
  transfers between devices with their start and end apart: 8, of which 5 were waited for; matrix products, arithmetic and copies ran while one was open for 1% of the time, Pallas kernels for 0%

profile of v1, /device:TPU:417, one launch (start us, length us, event | category | flops | bytes accessed | tf_op | source)
XLA Modules:
  0.0 510.0 jit_solution(15715607884456569641)
XLA Ops:
  6.6 3.9 tile.2
  10.4 21.0 %all-to-all-start = ((bf16[512,32,128]{2,0,1:T(8,128)(2,1)}), bf16[512,32,128]{2,0,1:T(8,128)(2,1)}, u32[]{:S(2)}, u32[]{:S(2)}) async-start(bf16[512,32,128]{2,0,1:T(8,128)(2,1)} %tile.2), calls=%async_computation | async-start | bytes 8388608 | tf_op jit(solution)/shard_map/all_to_all | solution.py:17
  33.6 182.1 %all-to-all-done = bf16[512,32,128]{2,0,1:T(8,128)(2,1)} async-done(((bf16[512,32,128]{2,0,1:T(8,128)(2,1)}), bf16[512,32,128]{2,0,1:T(8,128)(2,1)}, u32[]{:S(2)}, u32[]{:S(2)}) %all-to-all-start) | async-done | bytes 4194336 | tf_op jit(solution)/shard_map/all_to_all | solution.py:17
  215.7 6.5 %copy.36 = bf16[512,32,128]{0,2,1:T(8,128)(2,1)} copy(bf16[512,32,128]{2,0,1:T(8,128)(2,1)} %all-to-all-done) | data formatting | bytes 8388608 | tf_op jit(solution)/shard_map/all_to_all | solution.py:17
  222.2 3.6 convolution_convert_fusion
  225.8 1.6 broadcast_in_dim.51
  227.4 4.4 all-to-all-start.1
  233.8 22.7 %all-to-all-done.1 = bf16[4,64,4096]{2,1,0:T(8,128)(2,1)S(1)} async-done(((bf16[4,64,4096]{2,1,0:T(8,128)(2,1)}), bf16[4,64,4096]{2,1,0:T(8,128)(2,1)S(1)}, u32[]{:S(2)}, u32[]{:S(2)}) %all-to-all-start.1) | async-done | bytes 2097184 | tf_op jit(solution)/shard_map/all_to_all | solution.py:25
  258.4 78.2 %all-gather.3.cloned.1.call-done = bf16[32,36,4097]{2,1,0:T(8,128)(2,1)} async-done(((bf16[1,36,4097]{2,1,0:T(8,128)(2,1)}), bf16[32,36,4097]{2,1,0:T(8,128)(2,1)}) %all-gather.3.cloned.1.call-update) | async-done | bytes 9439504 | tf_op jit(solution)/shard_map/all_gather | solution.py:36
  336.6 14.2 %reshape.114 = bf16[1152,4097]{1,0:T(8,128)(2,1)} reshape(bf16[32,36,4097]{2,1,0:T(8,128)(2,1)} %all-gather.3.cloned.1.call-done) | data formatting | bytes 18878976
  352.0 9.8 %fusion.3 = f32[1152,448]{0,1:S(1)} fusion(bf16[4096,448]{0,1:T(8,128)(2,1)} %bitcast.72, bf16[1152,4097]{1,0:T(8,128)(2,1)} %reshape.114), kind=kOutput, calls=%fused_computation.4 | convolution fusion | flops 4227858432 | bytes 15171584
  361.8 4.9 fusion.1
  366.8 7.6 %bitcast_convert_fusion = bf16[1152,4096]{1,0:T(8,128)(2,1)} fusion(bf16[2,224,4096]{2,1,0:T(8,128)(2,1)S(1)} %copy-done.11, f32[2,1152,224]{1,2,0:T(8,128)S(1)} %bitcast.75, f32[2,1152,224]{1,2,0:T(8,128)S(1)} %bitcast.74, f32[2,1152]{1,0:T(2,128)S(1)} %pad_maximum_fusion), kind=kOutput, calls=%fused_computation.1 | convolution fusion | flops 4236189696 | bytes 17245184 | tf_op jit(solution)/shard_map/enf,efd->nd/dot_general | solution.py:120
  374.5 72.3 %fusion = bf16[40,4096]{1,0:T(8,128)(2,1)S(1)} fusion(bf16[1152,4096]{1,0:T(8,128)(2,1)} %bitcast_convert_fusion), kind=kCustom, calls=%all-reduce-scatter | all-reduce-scatter fusion | flops 5242881 | bytes 9765888
  446.8 5.8 %collective-permute-start = (bf16[40,4096]{1,0:T(8,128)(2,1)S(1)}, bf16[40,4096]{1,0:T(8,128)(2,1)S(1)}, u32[]{:S(2)}, u32[]{:S(2)}) collective-permute-start(bf16[40,4096]{1,0:T(8,128)(2,1)S(1)} %fusion), channel_id=1, source_target_pairs={{0,4},{4,8},{8,12},{12,16},{16,20},{20,24},{24,28},{28,32},{32,36}... | collective-permute-start | bytes 983048
  452.7 2.0 collective-permute-start.1
  454.6 2.0 collective-permute-start.2
  457.5 5.3 %collective-permute-start.3 = (bf16[4,4096]{1,0:T(4,128)(2,1)S(1)}, bf16[4,4096]{1,0:T(4,128)(2,1)S(1)}, u32[]{:S(2)}, u32[]{:S(2)}) collective-permute-start(bf16[4,4096]{1,0:T(4,128)(2,1)S(1)} %slice.20), channel_id=1, source_target_pairs={{0,16},{4,20},{8,24},{12,28},{16,32},{20,36},{24,40},{28,44},{32,4... | collective-permute-start | bytes 98312
  464.3 11.4 %collective-permute-done.3 = bf16[4,4096]{1,0:T(4,128)(2,1)S(1)} collective-permute-done((bf16[4,4096]{1,0:T(4,128)(2,1)S(1)}, bf16[4,4096]{1,0:T(4,128)(2,1)S(1)}, u32[]{:S(2)}, u32[]{:S(2)}) %collective-permute-start.3) | collective-permute-done | bytes 32800
  475.6 1.7 concatenate.4
  478.7 2.3 reshape.104
  481.0 5.3 %multiply_reduce_fusion = bf16[64,4096]{1,0:T(8,128)(2,1)S(1)} fusion(f32[64,2,4096]{2,1,0:T(2,128)} %reshape.104, pred[64,2]{1,0:T(8,128)(4,1)S(1)} %copy.38, f32[64,2]{1,0:T(8,128)S(1)} %copy.37), kind=kLoop, calls=%fused_computation.12 | loop fusion | flops 1310720 | bytes 2622080 | tf_op jit(solution)/shard_map/reduce_sum | solution.py:131
  487.6 4.0 all-to-all-start.2
  491.6 9.9 %all-to-all-done.2 = bf16[4,64,1024]{2,1,0:T(8,128)(2,1)S(1)} async-done(((bf16[4,64,1024]{2,1,0:T(8,128)(2,1)}), bf16[4,64,1024]{2,1,0:T(8,128)(2,1)S(1)}, u32[]{:S(2)}, u32[]{:S(2)}) %all-to-all-start.2) | async-done | bytes 524320 | tf_op jit(solution)/shard_map/all_to_all | solution.py:51
  (67 shorter events, 13.1 us)
Async XLA Ops:
  6.5 25.1 %copy-start = (bf16[1,2048,128]{2,1,0:T(8,128)(2,1)S(1)}, bf16[1,2048,128]{2,1,0:T(8,128)(2,1)}, u32[]{:S(2)}) copy-start(bf16[1,2048,128]{2,1,0:T(8,128)(2,1)} %param.13) | copy-start | bytes 1572868
  10.4 21.2 %copy-start.5 = (bf16[64,512]{1,0:T(8,128)(2,1)S(1)}, bf16[64,512]{1,0:T(8,128)(2,1)}, u32[]{:S(2)}) copy-start(bf16[64,512]{1,0:T(8,128)(2,1)} %param.12) | copy-start | bytes 196612
  10.4 205.2 %all-to-all-start = ((bf16[512,32,128]{2,0,1:T(8,128)(2,1)}), bf16[512,32,128]{2,0,1:T(8,128)(2,1)}, u32[]{:S(2)}, u32[]{:S(2)}) async-start(bf16[512,32,128]{2,0,1:T(8,128)(2,1)} %tile.2), calls=%async_computation | async-start | bytes 8388608 | tf_op jit(solution)/shard_map/all_to_all | solution.py:17
  31.6 1.1 copy-start.12
  227.4 4.4 copy-start.6
  227.4 5.7 %copy-start.8 = (s32[64,2]{0,1:T(2,128)S(1)}, s32[64,2]{0,1:T(2,128)}, u32[]{:S(2)}) copy-start(s32[64,2]{0,1:T(2,128)} %param.20) | copy-start | bytes 1540
  227.4 5.8 %copy-start.7 = (s32[64,2]{0,1:T(2,128)S(1)}, s32[64,2]{0,1:T(2,128)}, u32[]{:S(2)}) copy-start(s32[64,2]{0,1:T(2,128)} %param.19) | copy-start | bytes 1540
  227.4 29.2 %all-to-all-start.1 = ((bf16[4,64,4096]{2,1,0:T(8,128)(2,1)}), bf16[4,64,4096]{2,1,0:T(8,128)(2,1)S(1)}, u32[]{:S(2)}, u32[]{:S(2)}) async-start(bf16[4,64,4096]{2,1,0:T(8,128)(2,1)} %broadcast_in_dim.51), calls=%async_computation.1 | async-start | bytes 4194304 | tf_op jit(solution)/shard_map/all_to_all | solution.py:25
  231.8 25.1 %copy-start.4 = (bf16[64,4096]{1,0:T(8,128)(2,1)S(1)}, bf16[64,4096]{1,0:T(8,128)(2,1)}, u32[]{:S(2)}) copy-start(bf16[64,4096]{1,0:T(8,128)(2,1)} %param.16) | copy-start | bytes 1572868
  231.8 104.8 %all-gather.3.cloned.1.call-start = ((), (), s32[]{:S(2)}) async-start(), calls=%async_computation.3 | async-start | bytes 11151360 | tf_op jit(solution)/shard_map/all_gather | solution.py:36
  233.8 23.4 %copy-start.13 = (f32[4096]{0:T(1024)S(1)}, f32[4096]{0:T(1024)}, u32[]{:S(2)}) copy-start(f32[4096]{0:T(1024)} %param.17) | copy-start | bytes 49156
  257.2 93.7 %copy-start.3 = (bf16[64,4096]{1,0:T(8,128)(2,1)}, bf16[64,4096]{1,0:T(8,128)(2,1)S(1)}, u32[]{:S(2)}) copy-start(bf16[64,4096]{1,0:T(8,128)(2,1)S(1)} %get-tuple-element.10) | copy-start | bytes 1572868
  352.0 9.8 %copy-start.2 = (bf16[1152,4097]{1,0:T(8,128)(2,1)S(1)}, bf16[1152,4097]{1,0:T(8,128)(2,1)}, u32[]{:S(2)}) copy-start(bf16[1152,4097]{1,0:T(8,128)(2,1)} %reshape.114) | copy-start | bytes 28318468
  352.0 9.8 %copy-start.10 = (bf16[2,4096,224]{1,2,0:T(8,128)(2,1)S(1)}, bf16[2,4096,224]{1,2,0:T(8,128)(2,1)}, u32[]{:S(2)}) copy-start(bf16[2,4096,224]{1,2,0:T(8,128)(2,1)} %param.22) | copy-start | bytes 11010052
  361.8 5.0 copy-start.11
  374.4 88.6 %copy-start.9 = (u32[256]{0:T(256)S(1)}, u32[256]{0:T(256)}, u32[]{:S(2)}) copy-start(u32[256]{0:T(256)} %constant.60) | copy-start | bytes 3076
  446.8 28.8 %collective-permute-start = (bf16[40,4096]{1,0:T(8,128)(2,1)S(1)}, bf16[40,4096]{1,0:T(8,128)(2,1)S(1)}, u32[]{:S(2)}, u32[]{:S(2)}) collective-permute-start(bf16[40,4096]{1,0:T(8,128)(2,1)S(1)} %fusion), channel_id=1, source_target_pairs={{0,4},{4,8},{8,12},{12,16},{16,20},{20,24},{24,28},{28,32},{32,36}... | collective-permute-start | bytes 983048
  452.7 23.0 %collective-permute-start.1 = (bf16[40,4096]{1,0:T(8,128)(2,1)S(1)}, bf16[40,4096]{1,0:T(8,128)(2,1)S(1)}, u32[]{:S(2)}, u32[]{:S(2)}) collective-permute-start(bf16[40,4096]{1,0:T(8,128)(2,1)S(1)} %fusion), channel_id=1, source_target_pairs={{0,8},{4,12},{8,16},{12,20},{16,24},{20,28},{24,32},{28,36},{32,40... | collective-permute-start | bytes 983048
  454.6 21.0 %collective-permute-start.2 = (bf16[40,4096]{1,0:T(8,128)(2,1)S(1)}, bf16[40,4096]{1,0:T(8,128)(2,1)S(1)}, u32[]{:S(2)}, u32[]{:S(2)}) collective-permute-start(bf16[40,4096]{1,0:T(8,128)(2,1)S(1)} %fusion), channel_id=1, source_target_pairs={{0,12},{4,16},{8,20},{12,24},{16,28},{20,32},{24,36},{28,40},{32,4... | collective-permute-start | bytes 983048
  457.5 18.1 %collective-permute-start.3 = (bf16[4,4096]{1,0:T(4,128)(2,1)S(1)}, bf16[4,4096]{1,0:T(4,128)(2,1)S(1)}, u32[]{:S(2)}, u32[]{:S(2)}) collective-permute-start(bf16[4,4096]{1,0:T(4,128)(2,1)S(1)} %slice.20), channel_id=1, source_target_pairs={{0,16},{4,20},{8,24},{12,28},{16,32},{20,36},{24,40},{28,44},{32,4... | collective-permute-start | bytes 98312
  481.0 22.2 %copy-start.1 = (bf16[1,2048,128]{2,1,0:T(8,128)(2,1)S(1)}, bf16[1,2048,128]{2,1,0:T(8,128)(2,1)}, u32[]{:S(2)}) copy-start(bf16[1,2048,128]{2,1,0:T(8,128)(2,1)} %param.13) | copy-start | bytes 1572868
  487.6 13.9 %all-to-all-start.2 = ((bf16[4,64,1024]{2,1,0:T(8,128)(2,1)}), bf16[4,64,1024]{2,1,0:T(8,128)(2,1)S(1)}, u32[]{:S(2)}, u32[]{:S(2)}) async-start(bf16[4,64,1024]{2,1,0:T(8,128)(2,1)} %copy.40), calls=%async_computation.2 | async-start | bytes 1048576 | tf_op jit(solution)/shard_map/all_to_all | solution.py:51
Sparse Core Ops, SparseCore 0:
  258.5 78.0 all-gather.2
